TPU v7x, 32 devices: a whole 2x2x4 slice. The times are simulated.
32 devices in a mesh: rep: 2 (over x), dp: 16 (over y, z, core).
Axes of the slice: x: 2, y: 2, z: 4, core: 2. Of those that a mesh axis runs over, the one named last changes fastest.
Arguments:
- g_w_gate: bfloat16 [32, 2, 1024, 3072], P(('rep', 'dp')), parts along dimension 0
- g_w_up: bfloat16 [32, 2, 1024, 3072], P(('rep', 'dp')), parts along dimension 0
- g_w_down: bfloat16 [32, 2, 3072, 1024], P(('rep', 'dp')), parts along dimension 0
- w_gate: bfloat16 [2, 1024, 3072], replicated
- w_up: bfloat16 [2, 1024, 3072], replicated
- w_down: bfloat16 [2, 3072, 1024], replicated
- m_w_gate: float32 [2, 1024, 3072], P(None, 'dp')
- m_w_up: float32 [2, 1024, 3072], P(None, 'dp')
- m_w_down: float32 [2, 3072, 1024], P(None, 'dp')
- v_w_gate: float32 [2, 1024, 3072], P(None, 'dp')
- v_w_up: float32 [2, 1024, 3072], P(None, 'dp')
- v_w_down: float32 [2, 3072, 1024], P(None, 'dp')
Outputs:
- output 1: bfloat16 [4, 1024, 3072], P('rep'), parts along dimension 0
- output 2: bfloat16 [4, 1024, 3072], P('rep'), parts along dimension 0
- output 3: bfloat16 [4, 3072, 1024], P('rep'), parts along dimension 0
- output 4: float32 [4, 1024, 3072], P('rep', 'dp'), parts along dimension 0
- output 5: float32 [4, 1024, 3072], P('rep', 'dp'), parts along dimension 0
- output 6: float32 [4, 3072, 1024], P('rep', 'dp'), parts along dimension 0
- output 7: float32 [4, 1024, 3072], P('rep', 'dp'), parts along dimension 0
- output 8: float32 [4, 1024, 3072], P('rep', 'dp'), parts along dimension 0
- output 9: float32 [4, 3072, 1024], P('rep', 'dp'), parts along dimension 0
There are 2 independent parts. A program takes and returns all parts, laid end to end along the dimension named above; an argument that names none is the same for every part.
All inputs are finite; a program needn't handle non-finite values.
Results may differ from a plain program's by a relative error of at most 0.022.
Values are sent between devices in bfloat16 or wider.
A program may use at most 2 GiB of HBM per device.

v0:
```python
import jax
import jax.numpy as jnp
from jax import lax
from jax.sharding import PartitionSpec as P


def adamw(w, m, v, g):
    m = 0.9 * m + 0.1 * g
    v = 0.95 * v + 0.05 * g * g
    step = m * lax.rsqrt(v + 1e-8) + 0.1 * w
    return (w - 0.02 * step).astype(jnp.bfloat16), m, v


def solution(mesh):
    def step(*arrays):
        terms, weights, m, v = (arrays[i : i + 3] for i in (0, 3, 6, 9))
        gradients = [lax.psum_scatter(t[0], "dp", scatter_dimension=1, tiled=True).astype(jnp.float32) for t in terms]
        me = lax.axis_index("dp")
        own = [lax.dynamic_slice_in_dim(w, me * one.shape[1], one.shape[1], 1).astype(jnp.float32) for w, one in zip(weights, m, strict=True)]
        new = [adamw(w, m, v, g) for w, m, v, g in zip(own, m, v, gradients, strict=True)]
        whole = [lax.all_gather(one[0], "dp", axis=1, tiled=True) for one in new]
        return (*whole, *(one[1] for one in new), *(one[2] for one in new))

    all_of, cut = P(None, None, None), P(None, "dp", None)
    return jax.shard_map(
        step,
        mesh=mesh,
        in_specs=(P(("rep", "dp"), None, None, None),) * 3 + (all_of,) * 3 + (cut,) * 6,
        out_specs=(P("rep", None, None),) * 3 + (P("rep", "dp", None),) * 6,
        check_vma=False,
    )
```

profile of v0, /device:TPU:0, one launch (start us, length us, event | category | flops | bytes accessed | tf_op | source)
XLA Modules:
  0.0 760.0 jit_solution(13758306267096514254)
XLA Ops:
  7.2 0.0 reduce-scatter.8.cloned.1.call-start
  7.2 0.7 reduce-scatter.8.cloned.1.call-update
  7.9 0.0 reduce-scatter.6.cloned.1.call-start
  8.0 0.7 reduce-scatter.6.cloned.1.call-update
  8.7 0.0 reduce-scatter.4.cloned.1.call-start
  8.7 0.0 copy-start.1
  8.7 0.0 copy-start.2
  8.7 0.7 reduce-scatter.4.cloned.1.call-update
  9.4 0.0 all-gather.8.cloned.1.call-start
  9.4 138.8 %reduce-scatter.8.cloned.1.call-done = bf16[2,192,1024]{2,1,0:T(8,128)(2,1)} async-done(((bf16[2,3072,1024]{2,1,0:T(8,128)(2,1)}), bf16[2,192,1024]{2,1,0:T(8,128)(2,1)}) %reduce-scatter.8.cloned.1.call-update) | async-done | bytes 786448 | tf_op jit(solution)/shard_map/reduce_scatter | solution.py:17
  148.2 0.0 copy-done.1
  148.2 0.0 copy-done.2
  148.2 3.8 fusion.10
  152.0 0.0 all-gather.8.cloned.1.call-update
  152.0 0.0 all-gather.6.cloned.1.call-start
  152.0 133.2 %reduce-scatter.6.cloned.1.call-done = bf16[2,64,3072]{2,1,0:T(8,128)(2,1)} async-done(((bf16[2,1024,3072]{2,1,0:T(8,128)(2,1)}), bf16[2,64,3072]{2,1,0:T(8,128)(2,1)}) %reduce-scatter.6.cloned.1.call-update) | async-done | bytes 786448 | tf_op jit(solution)/shard_map/reduce_scatter | solution.py:17
  285.3 0.0 copy-start.3
  285.3 0.0 copy-start.4
  285.3 4.8 fusion.6
  290.1 0.0 all-gather.6.cloned.1.call-update
  290.1 0.0 all-gather.4.cloned.1.call-start
  290.2 132.2 %reduce-scatter.4.cloned.1.call-done = bf16[2,64,3072]{2,1,0:T(8,128)(2,1)} async-done(((bf16[2,1024,3072]{2,1,0:T(8,128)(2,1)}), bf16[2,64,3072]{2,1,0:T(8,128)(2,1)}) %reduce-scatter.4.cloned.1.call-update) | async-done | bytes 786448 | tf_op jit(solution)/shard_map/reduce_scatter | solution.py:17
  422.4 0.0 copy-done.3
  422.4 0.0 copy-done.4
  422.4 3.7 fusion.2
  426.1 0.0 all-gather.4.cloned.1.call-update
  426.1 98.7 %all-gather.8.cloned.1.call-done = bf16[2,3072,1024]{2,1,0:T(8,128)(2,1)} async-done(((bf16[2,192,1024]{2,1,0:T(8,128)(2,1)}), bf16[2,3072,1024]{2,1,0:T(8,128)(2,1)}) %all-gather.8.cloned.1.call-update) | async-done | bytes 12582928 | tf_op jit(solution)/shard_map/all_gather | solution.py:21
  524.8 101.2 %all-gather.6.cloned.1.call-done = bf16[2,1024,3072]{2,1,0:T(8,128)(2,1)} async-done(((bf16[2,64,3072]{2,1,0:T(8,128)(2,1)}), bf16[2,1024,3072]{2,1,0:T(8,128)(2,1)}) %all-gather.6.cloned.1.call-update) | async-done | bytes 12582928 | tf_op jit(solution)/shard_map/all_gather | solution.py:21
  626.0 101.2 %all-gather.4.cloned.1.call-done = bf16[2,1024,3072]{2,1,0:T(8,128)(2,1)} async-done(((bf16[2,64,3072]{2,1,0:T(8,128)(2,1)}), bf16[2,1024,3072]{2,1,0:T(8,128)(2,1)}) %all-gather.4.cloned.1.call-update) | async-done | bytes 12582928 | tf_op jit(solution)/shard_map/all_gather | solution.py:21
  727.2 0.0 copy-start
  727.2 0.0 slice-start
  727.2 0.0 slice-start.1
  727.2 12.4 %copy.24 = bf16[2,1024,3072]{2,1,0:T(8,128)(2,1)} copy(bf16[2,1024,3072]{2,1,0:T(8,128)(2,1)} %all-gather.4.cloned.1.call-done) | data formatting | bytes 25165824
  739.6 0.0 copy-done
  739.6 0.0 slice-start.2
  739.6 6.4 copy.25
  746.0 0.0 slice-done
  746.0 1.1 slice-done.1
  747.1 1.3 slice-done.2
  748.4 4.8 copy.26
  (1 shorter events, 0.0 us)
Async XLA Ops:
  7.2 141.0 %reduce-scatter.8.cloned.1.call-start = ((), (), s32[]{:S(2)}) async-start(), calls=%async_computation.7 | async-start | bytes 13369344 | tf_op jit(solution)/shard_map/reduce_scatter | solution.py:17
  7.9 277.4 %reduce-scatter.6.cloned.1.call-start = ((), (), s32[]{:S(2)}) async-start(), calls=%async_computation.5 | async-start | bytes 13369344 | tf_op jit(solution)/shard_map/reduce_scatter | solution.py:17
  8.7 413.7 %reduce-scatter.4.cloned.1.call-start = ((), (), s32[]{:S(2)}) async-start(), calls=%async_computation.3 | async-start | bytes 13369344 | tf_op jit(solution)/shard_map/reduce_scatter | solution.py:17
  8.7 139.5 %copy-start.1 = (f32[2,192,1024]{2,1,0:T(8,128)S(1)}, f32[2,192,1024]{2,1,0:T(8,128)}, u32[]{:S(2)}) copy-start(f32[2,192,1024]{2,1,0:T(8,128)} %param.23) | copy-start | bytes 4718596
  8.7 139.5 %copy-start.2 = (f32[2,192,1024]{2,1,0:T(8,128)S(1)}, f32[2,192,1024]{2,1,0:T(8,128)}, u32[]{:S(2)}) copy-start(f32[2,192,1024]{2,1,0:T(8,128)} %param.20) | copy-start | bytes 4718596
  9.4 515.4 %all-gather.8.cloned.1.call-start = ((), (), s32[]{:S(2)}) async-start(), calls=%async_computation.8 | async-start | bytes 13369344 | tf_op jit(solution)/shard_map/all_gather | solution.py:21
  152.0 474.0 %all-gather.6.cloned.1.call-start = ((), (), s32[]{:S(2)}) async-start(), calls=%async_computation.6 | async-start | bytes 13369344 | tf_op jit(solution)/shard_map/all_gather | solution.py:21
  285.3 137.1 %copy-start.3 = (f32[2,64,3072]{2,1,0:T(8,128)S(1)}, f32[2,64,3072]{2,1,0:T(8,128)}, u32[]{:S(2)}) copy-start(f32[2,64,3072]{2,1,0:T(8,128)} %param.21) | copy-start | bytes 4718596
  285.3 137.1 %copy-start.4 = (f32[2,64,3072]{2,1,0:T(8,128)S(1)}, f32[2,64,3072]{2,1,0:T(8,128)}, u32[]{:S(2)}) copy-start(f32[2,64,3072]{2,1,0:T(8,128)} %param.18) | copy-start | bytes 4718596
  290.1 437.0 %all-gather.4.cloned.1.call-start = ((), (), s32[]{:S(2)}) async-start(), calls=%async_computation.4 | async-start | bytes 13369344 | tf_op jit(solution)/shard_map/all_gather | solution.py:21
  727.2 12.4 %copy-start = (bf16[2,1024,3072]{2,1,0:T(8,128)(2,1)S(1)}, bf16[2,1024,3072]{2,1,0:T(8,128)(2,1)}, u32[]{:S(2)}) copy-start(bf16[2,1024,3072]{2,1,0:T(8,128)(2,1)} %all-gather.6.cloned.1.call-done) | copy-start | bytes 37748740
  727.2 18.8 %slice-start = ((s8[12582912]{0:T(1024)(128)(4,1)}), s8[4194304]{0:T(1024)(128)(4,1)S(1)}, s32[]{:S(2)}) async-start(s8[12582912]{0:T(1024)(128)(4,1)} %bitcast.6), calls=%async_computation.9 | async-start | bytes 8388608
  727.2 19.9 %slice-start.1 = ((s8[12582912]{0:T(1024)(128)(4,1)}), s8[4194304]{0:T(1024)(128)(4,1)S(1)}, s32[]{:S(2)}) async-start(s8[12582912]{0:T(1024)(128)(4,1)} %bitcast.6), calls=%async_computation.10 | async-start | bytes 8388608
  739.6 8.8 %slice-start.2 = ((s8[12582912]{0:T(1024)(128)(4,1)}), s8[4194304]{0:T(1024)(128)(4,1)S(1)}, s32[]{:S(2)}) async-start(s8[12582912]{0:T(1024)(128)(4,1)} %bitcast.6), calls=%async_computation.11 | async-start | bytes 8388608
Sparse Core Ops, SparseCore 0:
  12.0 136.1 reduce-scatter.7
  152.2 132.9 reduce-scatter.5
  289.3 132.9 reduce-scatter.3
  425.0 99.6 all-gather.7
  527.4 98.4 all-gather.5
  628.6 98.4 all-gather.3
where the time goes:
time: 760 us
  waiting for transfers between devices  707 us (93%)
  local copies, waits for them, and re-layouts  26 us (3%)
  between operations  14.2 us (2%)
  other arithmetic  12.3 us (2%)
    reduce_scatter x3, waiting for transfers between devices, step(): lax.psum_scatter(t[0], 'dp', scatter_dimension=1, tiled=True)  404 us
    all_gather x3, waiting for transfers between devices, step(): whole = [lax.all_gather(one[0], 'dp', axis=1, tiled=True) for one in new]  301 us
    unnamed x19, local copies, waits for them, and re-layouts  26 us
  transfers between devices with their start and end apart: 6, of which 6 were waited for; matrix products, arithmetic and copies ran while one was open for 2% of the time, Pallas kernels for 0%

commit v1 on v0

v1 whole, which is shorter than its diff:
```python
import functools

import jax
import jax.numpy as jnp
from jax import lax
from jax.experimental import pallas as pl
from jax.experimental.pallas import tpu as pltpu
from jax.sharding import PartitionSpec as P

MESH = pl.DeviceIdType.MESH
Y, Z = 2, 4
CUTS = 8
ACC = 9
STAGED = 4
STAGES = 10


def kernel(groups, cuts, acc_slots, *refs):
    terms, weights, moments_m, moments_v = (refs[i : i + 3] for i in (0, 3, 6, 9))
    whole, new_m, new_v = (refs[i : i + 3] for i in (12, 15, 18))
    acc_a, acc_b, all_a, all_b, y_a, y_b, z_a, z_b, w_a, w_b, m_a, m_b, v_a, v_b = refs[21:35]
    load_sem, pair_send, pair_recv, y_send, y_recv, z_send, z_recv, spread_send, spread_recv = refs[35:44]
    back_send, back_recv, out_send, out_recv, store_sem, state_sem, keep_sem = refs[44:51]

    rep, me = lax.axis_index("rep"), lax.axis_index("dp")
    c = lax.rem(me, 2)
    z = lax.rem(me // 2, Z)
    y = me // (2 * Z)
    far = Z - 1 - z
    partner = me + 1 - 2 * c
    across = me + (1 - 2 * y) * (2 * Z)
    beside = (me + 2, me - 2)
    place = (z, far)

    def send_to(device, src, dst, send_sem, recv_sem):
        return pltpu.make_async_remote_copy(
            src_ref=src, dst_ref=dst, send_sem=send_sem, recv_sem=recv_sem, device_id=(rep, device), device_id_type=MESH
        )

    def f32(x):
        return x.astype(jnp.float32)

    def own_load(g, k):
        layer, h, slot = g // cuts, lax.rem(g, cuts), lax.rem(g, acc_slots)
        dst = acc_b.at[slot] if k == 2 else acc_a.at[slot, k]
        return pltpu.make_async_copy(terms[k].at[layer, :, :, c, h], dst, load_sem.at[lax.rem(g, 4), k])

    def pair_copy(g, k):
        layer, h = g // cuts, lax.rem(g, cuts)
        dst = all_b.at[g] if k == 2 else all_a.at[g, k]
        return send_to(partner, terms[k].at[layer, :, :, 1 - c, h], dst, pair_send.at[lax.rem(g, 4), k], pair_recv.at[g, k])

    def y_copy(g, kind):
        slot = lax.rem(g, acc_slots)
        src, dst = (acc_b.at[slot, 1 - y, z], y_b.at[g]) if kind else (acc_a.at[slot, :, 1 - y], y_a.at[g])
        return send_to(across, src, dst, y_send.at[lax.rem(g, 2), kind], y_recv.at[g, kind])

    def z_copy(g, kind, way, s):
        slot = lax.rem(g, acc_slots)
        t = Z - 1 - s + z if way == 0 else s - far
        src, dst = (acc_b.at[slot, :, t], z_b.at[g, way, s]) if kind else (acc_a.at[slot, :, y, t], z_a.at[g, way, s])
        return send_to(beside[way], src, dst, z_send.at[lax.rem(g, 2), kind, way, s], z_recv.at[g, kind, way, s])

    def spread_copy(g, kind, way, s):
        t = z - s if way == 0 else z + s
        ref = all_b.at[g, :, t] if kind else all_a.at[g, :, y, t]
        return send_to(beside[way], ref, ref, spread_send.at[lax.rem(g, 2), kind, way, s], spread_recv.at[g, kind, way, s])

    def back_copy(g, kind):
        ref = all_b.at[g, y, z] if kind else all_a.at[g, :, y]
        return send_to(across, ref, ref, back_send.at[lax.rem(g, 2), kind], back_recv.at[g, kind])

    def out_parts(g, k, half):
        layer, h = g // cuts, lax.rem(g, cuts)
        if k == 2:
            return all_b.at[g], whole[k].at[layer, :, :, c, h], 4
        which = 1 - y if half else y
        return all_a.at[g, k, which], whole[k].at[layer, which, :, c, h], 2 * k + half

    def out_copy(g, k, half):
        src, dst, i = out_parts(g, k, half)
        return send_to(partner, src, dst, out_send.at[lax.rem(g, 2), i], out_recv.at[g, i])

    def out_store(g, k, half):
        src, dst, i = out_parts(g, k, half)
        return pltpu.make_async_copy(src, dst, store_sem.at[lax.rem(g, 2), i])

    def state_loads(g):
        layer, h, slot = g // cuts, lax.rem(g, cuts), lax.rem(g, STAGED)
        copies = []
        for k in range(3):
            w_ref, m_ref, v_ref = (w_b, m_b, v_b) if k == 2 else (w_a, m_a, v_a)
            at = (slot,) if k == 2 else (slot, k)
            copies.append(pltpu.make_async_copy(weights[k].at[layer, y, z, c, h], w_ref.at[at], state_sem.at[slot, 3 * k]))
            copies.append(pltpu.make_async_copy(moments_m[k].at[layer, h], m_ref.at[at], state_sem.at[slot, 3 * k + 1]))
            copies.append(pltpu.make_async_copy(moments_v[k].at[layer, h], v_ref.at[at], state_sem.at[slot, 3 * k + 2]))
        return copies

    def state_stores(g, kind):
        layer, h, slot = g // cuts, lax.rem(g, cuts), lax.rem(g, STAGED)
        copies = []
        for k in (2,) if kind else (0, 1):
            m_ref, v_ref = (m_b, v_b) if kind else (m_a, v_a)
            at = (slot,) if kind else (slot, k)
            copies.append(pltpu.make_async_copy(m_ref.at[at], new_m[k].at[layer, h], keep_sem.at[slot, 2 * k]))
            copies.append(pltpu.make_async_copy(v_ref.at[at], new_v[k].at[layer, h], keep_sem.at[slot, 2 * k + 1]))
        return copies

    def z_step(g, kind, s):
        slot = lax.rem(g, acc_slots)
        for way in (0, 1):
            t = Z - 1 - s + z if way == 0 else s - far

            def add(arrived, way=way, t=t):
                for i in (0, 1):
                    if kind:
                        total = f32(acc_b[slot, i, t]) + f32(all_b[g, i, t])
                        if arrived:
                            total += f32(z_b[g, way, s - 1, i])
                        acc_b[slot, i, t] = total.astype(jnp.bfloat16)
                    else:
                        total = f32(acc_a[slot, i, y, t]) + f32(all_a[g, i, y, t]) + f32(y_a[g, i, t])
                        if arrived:
                            total += f32(z_a[g, way, s - 1, i])
                        acc_a[slot, i, y, t] = total.astype(jnp.bfloat16)
                z_copy(g, kind, way, s).start()

            pl.when(place[way] == 0)(functools.partial(add, False))
            if s:
                pl.when((place[way] >= 1) & (place[way] <= s))(functools.partial(add, True))

    def z_wait(g, kind, s):
        for way in (0, 1):

            @pl.when((place[way] >= 1) & (place[way] <= s + 1))
            def _(way=way):
                ref = z_b.at[g, way, s] if kind else z_a.at[g, way, s]
                send_to(beside[way], ref, ref, z_send.at[0, kind, way, s], z_recv.at[g, kind, way, s]).wait_recv()

            @pl.when(place[way] <= s)
            def _(way=way):
                @pl.when(place[way] < Z - 1)
                def _():
                    z_copy(g, kind, way, s).wait_send()

    def spread_step(g, kind, s):
        for way in (0, 1):

            @pl.when((place[way] >= s) & (place[way] < Z - 1))
            def _(way=way):
                spread_copy(g, kind, way, s).start()

    def spread_wait(g, kind, s):
        for way in (0, 1):

            @pl.when(place[way] >= s + 1)
            def _(way=way):
                t = z - 1 - s if way == 0 else z + 1 + s
                ref = all_b.at[g, :, t] if kind else all_a.at[g, :, y, t]
                send_to(
                    beside[way], ref, ref, spread_send.at[lax.rem(g, 2), kind, way, s], spread_recv.at[g, kind, way, s]
                ).wait_recv()

            @pl.when((place[way] >= s) & (place[way] < Z - 1))
            def _(way=way):
                spread_copy(g, kind, way, s).wait_send()

    def arrived_along_z(up, down):
        up, down = f32(up), f32(down)
        return jnp.where(z >= 1, up, jnp.zeros_like(up)) + jnp.where(far >= 1, down, jnp.zeros_like(down))

    def adamw(total, w_ref, m_ref, v_ref, at):
        g = f32(total.astype(jnp.bfloat16))
        m = 0.9 * m_ref[at] + 0.1 * g
        v = 0.95 * v_ref[at] + 0.05 * g * g
        m_ref[at] = m
        v_ref[at] = v
        step = m * lax.rsqrt(v + 1e-8) + 0.1 * f32(w_ref[at])
        return f32(w_ref[at]) - 0.02 * step

    def stage_a(g, k):
        slot, staged = lax.rem(g, acc_slots), lax.rem(g, STAGED)
        if k == 1:
            for i in (0, 1):
                own_load(g, i).wait()
                pair_copy(g, i).wait_recv()
            for i in (0, 1):
                for t in range(Z):
                    acc_a[slot, i, 1 - y, t] = (f32(acc_a[slot, i, 1 - y, t]) + f32(all_a[g, i, 1 - y, t])).astype(jnp.bfloat16)
            y_copy(g, 0).start()
        if k == 2:
            for i in (0, 1):
                pair_copy(g, i).wait_send()
            y_copy(g, 0).wait()
            z_step(g, 0, 0)
        if k in (3, 4):
            z_wait(g, 0, k - 3)
            z_step(g, 0, k - 2)
        if k == 5:
            z_wait(g, 0, 2)
            for i in (0, 1):
                total = f32(acc_a[slot, i, y, z]) + f32(all_a[g, i, y, z]) + f32(y_a[g, i, z])
                total += arrived_along_z(z_a[g, 0, 2, i], z_a[g, 1, 2, i])
                all_a[g, i, y, z] = adamw(total, w_a, m_a, v_a, (staged, i)).astype(jnp.bfloat16)
            spread_step(g, 0, 0)
            for copy in state_stores(g, 0):
                copy.start()
        if k in (6, 7):
            spread_wait(g, 0, k - 6)
            spread_step(g, 0, k - 5)
        if k == 6:
            for copy in state_stores(g, 0):
                copy.wait()
        if k == 8:
            spread_wait(g, 0, 2)
            back_copy(g, 0).start()
            for i in (0, 1):
                out_copy(g, i, 0).start()
                out_store(g, i, 0).start()
        if k == 9:
            back_copy_recv = send_to(
                across, all_a.at[g, :, 1 - y], all_a.at[g, :, 1 - y], back_send.at[lax.rem(g, 2), 0], back_recv.at[g, 0]
            )
            back_copy_recv.wait_recv()
            back_copy(g, 0).wait_send()
            for i in (0, 1):
                out_copy(g, i, 1).start()
                out_store(g, i, 1).start()
        if k == 10:
            for i in (0, 1):
                for half in (0, 1):
                    out_copy(g, i, half).wait()
                    out_store(g, i, half).wait()

    def stage_b(g, k):
        slot, staged = lax.rem(g, acc_slots), lax.rem(g, STAGED)
        if k == 1:
            own_load(g, 2).wait()
            pair_copy(g, 2).wait_recv()
            z_step(g, 1, 0)
        if k == 2:
            pair_copy(g, 2).wait_send()
        if k in (2, 3):
            z_wait(g, 1, k - 2)
            z_step(g, 1, k - 1)
        if k == 4:
            z_wait(g, 1, 2)
            total = f32(acc_b[slot, 1 - y, z]) + f32(all_b[g, 1 - y, z])
            total += arrived_along_z(z_b[g, 0, 2, 1 - y], z_b[g, 1, 2, 1 - y])
            acc_b[slot, 1 - y, z] = total.astype(jnp.bfloat16)
            y_copy(g, 1).start()
        if k == 5:
            y_copy(g, 1).wait()
            total = f32(acc_b[slot, y, z]) + f32(all_b[g, y, z]) + f32(y_b[g])
            total += arrived_along_z(z_b[g, 0, 2, y], z_b[g, 1, 2, y])
            all_b[g, y, z] = adamw(total, w_b, m_b, v_b, (staged,)).astype(jnp.bfloat16)
            back_copy(g, 1).start()
            for copy in state_stores(g, 1):
                copy.start()
        if k == 6:
            for copy in state_stores(g, 1):
                copy.wait()
            send_to(
                across, all_b.at[g, 1 - y, z], all_b.at[g, 1 - y, z], back_send.at[lax.rem(g, 2), 1], back_recv.at[g, 1]
            ).wait_recv()
            back_copy(g, 1).wait_send()
            spread_step(g, 1, 0)
        if k in (7, 8):
            spread_wait(g, 1, k - 7)
            spread_step(g, 1, k - 6)
        if k == 9:
            spread_wait(g, 1, 2)
            out_copy(g, 2, 0).start()
            out_store(g, 2, 0).start()
        if k == 10:
            out_copy(g, 2, 0).wait()
            out_store(g, 2, 0).wait()

    def enter(g):
        for k in range(3):
            pair_copy(g, k).start()
        for k in range(3):
            own_load(g, k).start()

    barrier = pltpu.get_barrier_semaphore()
    for device in (partner, across):
        pl.semaphore_signal(barrier, inc=1, device_id=(rep, device), device_id_type=MESH)
    for way in (0, 1):

        @pl.when(place[way] < Z - 1)
        def _(way=way):
            pl.semaphore_signal(barrier, inc=1, device_id=(rep, beside[way]), device_id_type=MESH)

    pl.semaphore_wait(barrier, 4 - jnp.where(z == 0, 1, 0) - jnp.where(far == 0, 1, 0))

    enter(0)
    enter(1)

    @pl.loop(0, groups + STAGES - 1)
    def _(tick):
        for k in range(STAGES, 0, -1):
            g = tick - (k - 1)

            @pl.when((g >= 0) & (g < groups))
            def _(g=g, k=k):
                if k == 5:
                    for copy in state_loads(g):
                        copy.wait()
                stage_a(g, k)
                stage_b(g, k)
                if k == 3:
                    for copy in state_loads(g):
                        copy.start()

        @pl.when(tick + 2 < groups)
        def _():
            enter(tick + 2)


def update(terms, weights, m, v, cuts=CUTS):
    layers = weights[0].shape[0]
    groups = layers * cuts
    acc_slots = min(ACC, groups)
    full, own = [], []
    for w in weights:
        rows = w.shape[1] // (2 * Y * Z * cuts)
        full.append((layers, Y, Z, 2, cuts, rows, w.shape[2]))
        own.append((layers, cuts, rows, w.shape[2]))
    a, b = full[0][-2:], full[2][-2:]
    bf16, dma = jnp.bfloat16, pltpu.SemaphoreType.DMA
    anywhere = pl.BlockSpec(memory_space=pl.ANY)
    out = pl.pallas_call(
        functools.partial(kernel, groups, cuts, acc_slots),
        out_shape=[jax.ShapeDtypeStruct(s, bf16) for s in full] + [jax.ShapeDtypeStruct(s, jnp.float32) for s in own] * 2,
        in_specs=[anywhere] * 12,
        out_specs=[anywhere] * 9,
        scratch_shapes=[
            pltpu.VMEM((acc_slots, 2, Y, Z, *a), bf16),
            pltpu.VMEM((acc_slots, Y, Z, *b), bf16),
            pltpu.VMEM((groups, 2, Y, Z, *a), bf16),
            pltpu.VMEM((groups, Y, Z, *b), bf16),
            pltpu.VMEM((groups, 2, Z, *a), bf16),
            pltpu.VMEM((groups, *b), bf16),
            pltpu.VMEM((groups, 2, Z - 1, 2, *a), bf16),
            pltpu.VMEM((groups, 2, Z - 1, Y, *b), bf16),
            pltpu.VMEM((STAGED, 2, *a), bf16),
            pltpu.VMEM((STAGED, *b), bf16),
            *[pltpu.VMEM((STAGED, *s), jnp.float32) for _ in range(2) for s in ((2, *a), b)],
            dma((4, 3)),
            dma((4, 3)),
            dma((groups, 3)),
            dma((2, 2)),
            dma((groups, 2)),
            dma((2, 2, 2, Z - 1)),
            dma((groups, 2, 2, Z - 1)),
            dma((2, 2, 2, Z - 1)),
            dma((groups, 2, 2, Z - 1)),
            dma((2, 2)),
            dma((groups, 2)),
            dma((2, 5)),
            dma((groups, 5)),
            dma((2, 5)),
            dma((STAGED, 9)),
            dma((STAGED, 6)),
        ],
        compiler_params=pltpu.CompilerParams(collective_id=0, has_side_effects=True, vmem_limit_bytes=66_000_000),
        name="sum_step_spread",
    )(
        *[t.reshape(s) for t, s in zip(terms, full, strict=True)],
        *[w.reshape(s) for w, s in zip(weights, full, strict=True)],
        *[x.reshape(s) for x, s in zip(m, own, strict=True)],
        *[x.reshape(s) for x, s in zip(v, own, strict=True)],
    )
    return (
        *[o.reshape(w.shape) for o, w in zip(out[:3], weights, strict=True)],
        *[o.reshape(x.shape) for o, x in zip(out[3:6], m, strict=True)],
        *[o.reshape(x.shape) for o, x in zip(out[6:], v, strict=True)],
    )


def solution(mesh):
    def step(*arrays):
        terms, weights, m, v = (arrays[i : i + 3] for i in (0, 3, 6, 9))
        return update([t[0] for t in terms], weights, m, v)

    all_of, cut = P(None, None, None), P(None, "dp", None)
    return jax.shard_map(
        step,
        mesh=mesh,
        in_specs=(P(("rep", "dp"), None, None, None),) * 3 + (all_of,) * 3 + (cut,) * 6,
        out_specs=(P("rep", None, None),) * 3 + (P("rep", "dp", None),) * 6,
        check_vma=False,
    )
```

time: 760 us -> 383 us (0.50)
  waiting for transfers between devices: 707 us -> 0 us
  Pallas kernels: 0 us -> 345 us
  between operations: 14.2 us -> 0.69 us
  other arithmetic: 12.3 us -> 0.01 us
  local copies, waits for them, and re-layouts: 26 us -> 37 us
    reduce_scatter x3 -> x0, waiting for transfers between devices: 404 us -> none  [step(): lax.psum_scatter(t[0], 'dp', scatter_dimension=1, tiled=True)]
    pallas_call x0 -> x1, Pallas kernels: none -> 345 us  [update(): pl.pallas_call(functools.partial(kernel, groups, cuts, acc_slots), out_sh...]
    all_gather x3 -> x0, waiting for transfers between devices: 301 us -> none  [step(): whole = [lax.all_gather(one[0], 'dp', axis=1, tiled=True) for one in new]]
    convert_element_type x3 -> x0, other arithmetic: 12.3 us -> none  [adamw(): return ((w - 0.02 * step).astype(jnp.bfloat16), m, v)]
    unnamed x19 -> x29, local copies, waits for them, and re-layouts: 26 us -> 37 us
  transfers between devices with their start and end apart: 6 -> 0, of which waited for: 6 -> 0; matrix products, arithmetic and copies ran while one was open for 2% -> 0% of each run, Pallas kernels for 0% -> 0%
where the time goes in v1:
time: 383 us; the launch traced here: 382 us
  Pallas kernels  345 us (90%)
  local copies, waits for them, and re-layouts  37 us (10%)
    pallas_call x1, Pallas kernels, update(): pl.pallas_call(functools.partial(kernel, groups, cuts, acc_slots), out_sh...  345 us
    unnamed x29, local copies, waits for them, and re-layouts  37 us

profile of v1, /device:TPU:0, one launch (start us, length us, event | category | flops | bytes accessed | tf_op | source)
XLA Modules:
  0.0 382.3 jit_solution(5249791282535051590)
XLA Ops:
  0.6 344.6 %sum_step_spread.1 = (bf16[2,2,4,2,8,8,3072]{6,5,4,3,2,1,0:T(8,128)(2,1)}, bf16[2,2,4,2,8,8,3072]{6,5,4,3,2,1,0:T(8,128)(2,1)}, bf16[2,2,4,2,8,24,1024]{6,5,4,3,...) custom-call(bf16[2,2,4,2,8,8,3072]{6,5,4,3,2,1,0:T(8,128)(2,1)} %bit, ...), custom_call_target="tpu_custom_call" | custom-call | tf_op jit(solution)/shard_map/sum_step_spread/pallas_call | solution.py:332
  345.3 0.0 copy-start
  345.3 0.0 slice-start
  345.3 0.0 slice-start.1
  345.3 12.4 %copy.30 = bf16[2,1024,3072]{2,1,0:T(8,128)(2,1)} copy(bf16[2,1024,3072]{2,1,0:T(8,128)(2,1)} %bitcast.25) | data formatting | bytes 25165824
  357.7 0.0 copy-done
  357.7 0.0 slice-start.2
  357.7 6.4 %copy.31 = bf16[2,1024,3072]{2,1,0:T(8,128)(2,1)} copy(bf16[2,1024,3072]{2,1,0:T(8,128)(2,1)S(1)} %bitcast.24) | data formatting | bytes 25165824
  364.1 0.0 slice-done
  364.1 1.0 slice-done.1
  365.1 1.3 slice-done.2
  366.5 0.0 copy-start.6
  366.5 4.8 %copy.32 = bf16[2,3072,1024]{2,1,0:T(8,128)(2,1)} copy(bf16[2,3072,1024]{2,1,0:T(8,128)(2,1)S(1)} %bitcast.23) | data formatting | bytes 25165824
  371.2 0.0 copy-done.6
  371.2 0.0 copy-start.5
  371.2 1.1 copy.33
  372.4 0.8 copy-done.5
  373.2 0.0 copy-start.4
  373.2 1.1 copy.34
  374.4 0.8 copy-done.4
  375.2 0.0 copy-start.3
  375.2 1.1 copy.35
  376.3 0.8 copy-done.3
  377.2 0.0 copy-start.2
  377.2 1.1 copy.36
  378.3 0.8 copy-done.2
  379.1 0.0 copy-start.1
  379.1 1.1 copy.37
  380.3 0.8 copy-done.1
  381.1 1.1 copy.38
  (1 shorter events, 0.0 us)
Async XLA Ops:
  345.3 12.5 %copy-start = (bf16[2,2,4,2,8,8,3072]{6,5,4,3,2,1,0:T(8,128)(2,1)S(1)}, bf16[2,2,4,2,8,8,3072]{6,5,4,3,2,1,0:T(8,128)(2,1)}, u32[]{:S(2)}) copy-start(bf16[2,2,4,2,8,8,3072]{6,5,4,3,2,1,0:T(8,128)(2,1)} %get-tuple-element.19) | copy-start | bytes 37748740
  345.3 18.8 %slice-start = ((s8[12582912]{0:T(1024)(128)(4,1)}), s8[4194304]{0:T(1024)(128)(4,1)S(1)}, s32[]{:S(2)}) async-start(s8[12582912]{0:T(1024)(128)(4,1)} %bitcast.21), calls=%async_computation | async-start | bytes 8388608
  345.3 19.9 %slice-start.1 = ((s8[12582912]{0:T(1024)(128)(4,1)}), s8[4194304]{0:T(1024)(128)(4,1)S(1)}, s32[]{:S(2)}) async-start(s8[12582912]{0:T(1024)(128)(4,1)} %bitcast.21), calls=%async_computation.1 | async-start | bytes 8388608
  357.7 8.7 %slice-start.2 = ((s8[12582912]{0:T(1024)(128)(4,1)}), s8[4194304]{0:T(1024)(128)(4,1)S(1)}, s32[]{:S(2)}) async-start(s8[12582912]{0:T(1024)(128)(4,1)} %bitcast.21), calls=%async_computation.2 | async-start | bytes 8388608
  366.5 4.8 %copy-start.6 = (f32[2,8,8,3072]{3,2,1,0:T(8,128)S(1)}, f32[2,8,8,3072]{3,2,1,0:T(8,128)}, u32[]{:S(2)}) copy-start(f32[2,8,8,3072]{3,2,1,0:T(8,128)} %get-tuple-element.21) | copy-start | bytes 4718596
  371.2 2.0 copy-start.5
  373.2 2.0 copy-start.4
  375.2 2.0 copy-start.3
  377.2 2.0 copy-start.2
  379.1 2.0 copy-start.1

commit v2 on v0

v2 whole, which is shorter than its diff:
```python
import functools

import jax
import jax.numpy as jnp
from jax import lax
from jax.experimental import pallas as pl
from jax.experimental.pallas import tpu as pltpu
from jax.sharding import PartitionSpec as P

MESH = pl.DeviceIdType.MESH
Y, Z = 2, 4
ROWS, COLS = 8, 2
ACC = 6
SLOTS = 10
Y_SLOTS, UP_SLOTS, DOWN_SLOTS = 9, 5, 7
STAGED = 4
STAGES = 10
PAIR, DOWN, GATE, UP = range(4)
APART = (0, 10, 16, 22)
VMEM_BYTES = 13 * 2**20
PUT_BYTES = 13 * 2**20
ORDER = (
    (0, 1), (1, 1), (1, 2), (0, 8), (1, 3), (1, 4), (0, 7), (0, 10), (0, 9), (1, 9), (1, 8), (0, 4), (1, 7), (1, 10), (1, 5), (0, 6), (0, 3), (1, 6), (0, 5), (0, 2),
)


def kernel(groups, rows, cols, apart, *refs):
    terms, weights, moments_m, moments_v = (refs[i : i + 3] for i in (0, 3, 6, 9))
    mine_a, mine_b, theirs_a, theirs_b = refs[12:16]
    new_m, new_v = refs[16:19], refs[19:22]
    acc_a, acc_b, y_a, y_b, y_c, z_a, z_b, z_c, w_a, w_b, m_a, m_b, v_a, v_b = refs[22:36]
    load_sem, pair_send, pair_recv, y_send, y_recv, z_send, z_recv, spread_send, spread_recv = refs[36:45]
    back_send, back_recv, out_send, out_recv, state_sem, keep_sem = refs[45:51]

    rep, me = lax.axis_index("rep"), lax.axis_index("dp")
    c = lax.rem(me, 2)
    z = lax.rem(me // 2, Z)
    y = me // (2 * Z)
    far = Z - 1 - z
    partner = me + 1 - 2 * c
    across = me + (1 - 2 * y) * (2 * Z)
    beside = (me + 2, me - 2)
    place = (z, far)

    def send_to(device, src, dst, send_sem, recv_sem):
        return pltpu.make_async_remote_copy(
            src_ref=src, dst_ref=dst, send_sem=send_sem, recv_sem=recv_sem, device_id=(rep, device), device_id_type=MESH
        )

    def f32(x):
        return x.astype(jnp.float32)

    def part(g, ref):
        width = ref.shape[-1] // cols
        h = lax.rem(g, rows * cols)
        return g // (rows * cols), h // cols, pl.ds(pl.multiple_of(lax.rem(h, cols) * width, width), width)

    def z_first(kind):
        return kind in (DOWN, UP)

    def which(kind):
        return pl.ds(0, 2) if kind == PAIR else pl.ds(0, 1) if kind == GATE else 1

    def new_at(g, kind, *at, theirs=False):
        ref = (theirs_b if theirs else mine_b) if kind == DOWN else theirs_a if theirs else mine_a
        layer, h, width = part(g, ref)
        return ref.at[layer, *at, h, :, width] if kind == DOWN else ref.at[which(kind), layer, *at, h, :, width]

    def new_index(g, weight, i, t):
        layer, h, width = part(g, mine_b if weight == 2 else mine_a)
        return (layer, i, t, h, slice(None), width) if weight == 2 else (weight, layer, i, t, h, slice(None), width)

    def acc_at(g, kind, *at):
        slot = lax.rem(g, ACC)
        return acc_b.at[slot, *at] if kind == DOWN else acc_a.at[slot, which(kind), *at]

    def summed(g, weight, i, t):
        slot, here = lax.rem(g, ACC), new_index(g, weight, i, t)
        if weight == 2:
            return f32(acc_b[slot, i, t]) + f32(mine_b[here])
        return f32(acc_a[slot, weight, i, t]) + f32(mine_a[here])

    def keep(g, weight, i, t, total):
        slot = lax.rem(g, ACC)
        if weight == 2:
            acc_b[slot, i, t] = total.astype(jnp.bfloat16)
        else:
            acc_a[slot, weight, i, t] = total.astype(jnp.bfloat16)

    def own_load(g, k):
        layer, h, width = part(g, terms[k])
        dst = acc_b.at[lax.rem(g, ACC)] if k == 2 else acc_a.at[lax.rem(g, ACC), k]
        return pltpu.make_async_copy(terms[k].at[layer, :, :, c, h, :, width], dst, load_sem.at[lax.rem(g, 4), k])

    def pair_copy(g, k):
        layer, h, width = part(g, terms[k])
        src = terms[k].at[layer, :, :, 1 - c, h, :, width]
        dst = mine_b.at[layer, :, :, h, :, width] if k == 2 else mine_a.at[k, layer, :, :, h, :, width]
        return send_to(partner, src, dst, pair_send.at[lax.rem(g, 4), k], pair_recv.at[lax.rem(g, SLOTS), k])

    def slot_of(g, kind):
        if kind == DOWN:
            return lax.rem(g, DOWN_SLOTS)
        return lax.rem(sum(jnp.where(g > one, 1, 0) for one in apart), 2) if kind == UP else lax.rem(g, UP_SLOTS)

    def y_copy(g, kind):
        slot = lax.rem(g, SLOTS)
        if z_first(kind):
            src, dst = acc_at(g, kind, 1 - y, z), (y_b if kind == DOWN else y_c).at[slot_of(g, kind)]
        else:
            src, dst = acc_at(g, kind, 1 - y), y_a.at[lax.rem(g, Y_SLOTS), which(kind)]
        i = kind % 2 + kind // 3
        return send_to(across, src, dst, y_send.at[lax.rem(g, 2), i], y_recv.at[slot, i])

    def z_slot(g, kind, way, s):
        slot = slot_of(g, kind)
        if kind == DOWN:
            return z_b.at[slot, way, s]
        return z_c.at[slot, way, s] if kind == UP else z_a.at[slot, way, s, which(kind)]

    def z_copy(g, kind, way, s):
        t = Z - 1 - s + z if way == 0 else s - far
        src = acc_at(g, kind, slice(None), t) if z_first(kind) else acc_at(g, kind, y, t)
        i = kind % 2 + kind // 3
        sems = z_send.at[lax.rem(g, 2), i, way, s], z_recv.at[lax.rem(g, SLOTS), i, way, s]
        return send_to(beside[way], src, z_slot(g, kind, way, s), *sems)

    def spread_copy(g, kind, way, s, t):
        ref = new_at(g, kind, slice(None) if z_first(kind) else y, t)
        i = kind % 2 + kind // 3
        sems = spread_send.at[lax.rem(g, 2), i, way, s], spread_recv.at[lax.rem(g, SLOTS), i, way, s]
        return send_to(beside[way], ref, ref, *sems)

    def back_copy(g, kind, i, t):
        ref = new_at(g, kind, i, t)
        at = Z + kind // 3 if z_first(kind) else t
        return send_to(across, ref, ref, back_send.at[lax.rem(g, 2), at], back_recv.at[lax.rem(g, SLOTS), at])

    def out_copy(g, kind, half):
        at = slice(None) if z_first(kind) else 1 - y if half else y
        i = 2 + kind // 3 if z_first(kind) else half
        src, dst = new_at(g, kind, at, slice(None)), new_at(g, kind, at, slice(None), theirs=True)
        return send_to(partner, src, dst, out_send.at[lax.rem(g, 2), i], out_recv.at[lax.rem(g, SLOTS), i])

    def staged(g, k):
        slot = lax.rem(g, STAGED)
        return (w_b.at[slot], m_b.at[slot], v_b.at[slot]) if k == 2 else (w_a.at[slot, k], m_a.at[slot, k], v_a.at[slot, k])

    def state_loads(g, some):
        slot, copies = lax.rem(g, STAGED), []
        for k in some:
            layer, h, width = part(g, weights[k])
            w_ref, m_ref, v_ref = staged(g, k)
            copies.append(pltpu.make_async_copy(weights[k].at[layer, y, z, c, h, :, width], w_ref, state_sem.at[slot, 3 * k]))
            copies.append(pltpu.make_async_copy(moments_m[k].at[layer, h, :, width], m_ref, state_sem.at[slot, 3 * k + 1]))
            copies.append(pltpu.make_async_copy(moments_v[k].at[layer, h, :, width], v_ref, state_sem.at[slot, 3 * k + 2]))
        return copies

    def state_stores(g, k):
        layer, h, width = part(g, moments_m[k])
        _, m_ref, v_ref = staged(g, k)
        sems = keep_sem.at[lax.rem(g, STAGED), 2 * k], keep_sem.at[lax.rem(g, STAGED), 2 * k + 1]
        return (
            pltpu.make_async_copy(m_ref, new_m[k].at[layer, h, :, width], sems[0]),
            pltpu.make_async_copy(v_ref, new_v[k].at[layer, h, :, width], sems[1]),
        )

    def z_step(g, kind, s):
        slot = slot_of(g, kind)
        for way in (0, 1):
            t = Z - 1 - s + z if way == 0 else s - far

            def add(arrived, way=way, t=t):
                if z_first(kind):
                    weight = 2 if kind == DOWN else 1
                    came = z_b if kind == DOWN else z_c
                    for i in range(Y):
                        total = summed(g, weight, i, t)
                        if arrived:
                            total += f32(came[slot, way, s - 1, i])
                        keep(g, weight, i, t, total)
                else:
                    for weight in (0, 1) if kind == PAIR else (0,):
                        total = summed(g, weight, y, t) + f32(y_a[lax.rem(g, Y_SLOTS), weight, t])
                        if arrived:
                            total += f32(z_a[slot, way, s - 1, weight])
                        keep(g, weight, y, t, total)
                z_copy(g, kind, way, s).start()

            pl.when(place[way] == 0)(functools.partial(add, False))
            if s:
                pl.when((place[way] >= 1) & (place[way] <= s))(functools.partial(add, True))

    def z_wait(g, kind, s):
        i = kind % 2 + kind // 3
        for way in (0, 1):

            @pl.when((place[way] >= 1) & (place[way] <= s + 1))
            def _(way=way):
                ref = z_slot(g, kind, way, s)
                send_to(beside[way], ref, ref, z_send.at[0, i, way, s], z_recv.at[lax.rem(g, SLOTS), i, way, s]).wait_recv()

            @pl.when((place[way] <= s) & (place[way] < Z - 1))
            def _(way=way):
                z_copy(g, kind, way, s).wait_send()

    def spread_step(g, kind, s):
        for way in (0, 1):

            @pl.when((place[way] >= s) & (place[way] < Z - 1))
            def _(way=way):
                spread_copy(g, kind, way, s, z - s if way == 0 else z + s).start()

    def spread_wait(g, kind, s):
        for way in (0, 1):

            @pl.when(place[way] >= s + 1)
            def _(way=way):
                t = z - 1 - s if way == 0 else z + 1 + s
                spread_copy(g, kind, way, s, t).wait_recv()
                if not z_first(kind):
                    back_copy(g, kind, y, t).start()

            @pl.when((place[way] >= s) & (place[way] < Z - 1))
            def _(way=way):
                spread_copy(g, kind, way, s, z - s if way == 0 else z + s).wait_send()

    def along_z(came, g, kind, *at):
        slot = slot_of(g, kind)
        up, down = f32(came[slot, 0, Z - 2, *at]), f32(came[slot, 1, Z - 2, *at])
        return jnp.where(z >= 1, up, jnp.zeros_like(up)) + jnp.where(far >= 1, down, jnp.zeros_like(down))

    def adamw(g, weight, total):
        w_ref, m_ref, v_ref = staged(g, weight)
        w = f32(w_ref[...])
        gradient = f32(total.astype(jnp.bfloat16))
        m = 0.9 * m_ref[...] + 0.1 * gradient
        v = 0.95 * v_ref[...] + 0.05 * gradient * gradient
        m_ref[...] = m
        v_ref[...] = v
        new = (w - 0.02 * (m * lax.rsqrt(v + 1e-8) + 0.1 * w)).astype(jnp.bfloat16)
        if weight == 2:
            mine_b[new_index(g, weight, y, z)] = new
        else:
            mine_a[new_index(g, weight, y, z)] = new

    def y_first_stage(g, kind, k):
        some = (0, 1) if kind == PAIR else (0,)
        if k == 1:
            for i in some:
                own_load(g, i).wait()
                pair_copy(g, i).wait_recv()
            for i in some:
                for t in range(Z):
                    keep(g, i, 1 - y, t, summed(g, i, 1 - y, t))
            y_copy(g, kind).start()
        if k == 2:
            for i in some:
                pair_copy(g, i).wait_send()
            y_copy(g, kind).wait()
            z_step(g, kind, 0)
        if k in (3, 4):
            z_wait(g, kind, k - 3)
            z_step(g, kind, k - 2)
        if k == 5:
            z_wait(g, kind, 2)
            for i in some:
                adamw(g, i, summed(g, i, y, z) + f32(y_a[lax.rem(g, Y_SLOTS), i, z]) + along_z(z_a, g, kind, i))
            spread_step(g, kind, 0)
            back_copy(g, kind, y, z).start()
            for i in some:
                for copy in state_stores(g, i):
                    copy.start()
        if k in (6, 7):
            spread_wait(g, kind, k - 6)
            spread_step(g, kind, k - 5)
        if k == 6:
            for i in some:
                for copy in state_stores(g, i):
                    copy.wait()
        if k == 8:
            spread_wait(g, kind, 2)
            out_copy(g, kind, 0).start()
        if k == 9:
            for t in range(Z):
                back_copy(g, kind, 1 - y, t).wait_recv()
                back_copy(g, kind, y, t).wait_send()
            out_copy(g, kind, 1).start()
        if k == 10:
            for half in (0, 1):
                out_copy(g, kind, half).wait()

    def z_first_stage(g, kind, k):
        weight = 2 if kind == DOWN else 1
        came = z_b if kind == DOWN else z_c
        if k == 1:
            own_load(g, weight).wait()
            pair_copy(g, weight).wait_recv()
            z_step(g, kind, 0)
        if k == 2:
            pair_copy(g, weight).wait_send()
        if k in (2, 3):
            z_wait(g, kind, k - 2)
            z_step(g, kind, k - 1)
        if k == 4:
            z_wait(g, kind, 2)
            keep(g, weight, 1 - y, z, summed(g, weight, 1 - y, z) + along_z(came, g, kind, 1 - y))
            y_copy(g, kind).start()
        if k == 5:
            y_copy(g, kind).wait()
            arrived = f32((y_b if kind == DOWN else y_c)[slot_of(g, kind)])
            adamw(g, weight, summed(g, weight, y, z) + arrived + along_z(came, g, kind, y))
            back_copy(g, kind, y, z).start()
            for copy in state_stores(g, weight):
                copy.start()
        if k == 6:
            back_copy(g, kind, 1 - y, z).wait_recv()
            back_copy(g, kind, y, z).wait_send()
            spread_step(g, kind, 0)
            for copy in state_stores(g, weight):
                copy.wait()
        if k in (7, 8):
            spread_wait(g, kind, k - 7)
            spread_step(g, kind, k - 6)
        if k == 9:
            spread_wait(g, kind, 2)
            out_copy(g, kind, 0).start()
        if k == 10:
            out_copy(g, kind, 0).wait()

    def is_apart(g):
        found = g < 0
        for one in apart:
            found = found | (g == one)
        return found

    def enter(g):
        for k in range(3):
            pair_copy(g, k).start()
        for k in range(3):
            own_load(g, k).start()

    barrier = pltpu.get_barrier_semaphore()
    for device in (partner, across):
        pl.semaphore_signal(barrier, inc=1, device_id=(rep, device), device_id_type=MESH)
    for way in (0, 1):

        @pl.when(place[way] < Z - 1)
        def _(way=way):
            pl.semaphore_signal(barrier, inc=1, device_id=(rep, beside[way]), device_id_type=MESH)

    pl.semaphore_wait(barrier, 4 - jnp.where(z == 0, 1, 0) - jnp.where(far == 0, 1, 0))

    enter(0)
    enter(1)

    @pl.loop(0, groups + STAGES - 1)
    def _(tick):
        for kind, k in ORDER:
            g = tick - (k - 1)

            @pl.when((g >= 0) & (g < groups))
            def _(g=g, k=k, kind=kind):
                if k == 3 or k == 5:
                    for copy in state_loads(g, (2,) if kind else (0, 1)):
                        if k == 3:
                            copy.start()
                        else:
                            copy.wait()
                if kind == 1:
                    z_first_stage(g, DOWN, k)
                elif apart:
                    here = is_apart(g)

                    @pl.when(jnp.logical_not(here))
                    def _():
                        y_first_stage(g, PAIR, k)

                    @pl.when(here)
                    def _():
                        y_first_stage(g, GATE, k)
                        z_first_stage(g, UP, k)

                else:
                    y_first_stage(g, PAIR, k)

        @pl.when(tick + 2 < groups)
        def _():
            enter(tick + 2)


def put(*refs):
    halves, moments = (refs[0:2], refs[2:4]), refs[4:10]
    outs, rooms, sem = refs[10:19], refs[19:25], refs[25]
    c = lax.rem(lax.axis_index("dp"), 2)
    pairs = []
    for core, (a, b) in zip((c, 1 - c), halves, strict=True):
        for layer in range(b.shape[0]):
            sources = a.at[0, layer], a.at[1, layer], b.at[layer]
            pairs += [(src, out.at[layer, :, :, core]) for src, out in zip(sources, outs[:3], strict=True)]
    came = [pltpu.make_async_copy(src, room, sem.at[n]) for n, (src, room) in enumerate(zip(moments, rooms, strict=True))]
    gone = [pltpu.make_async_copy(room, out, sem.at[6 + n]) for n, (room, out) in enumerate(zip(rooms, outs[3:], strict=True))]
    copies = [pltpu.make_async_copy(src, dst, sem.at[12 + n]) for n, (src, dst) in enumerate(pairs)]
    for copy in came + copies:
        copy.start()
    for first, then in zip(came, gone, strict=True):
        first.wait()
        then.start()
    for copy in copies + gone:
        copy.wait()


def in_hbm(x):
    return pltpu.with_memory_space_constraint(x, pltpu.HBM)


def update(terms, weights, m, v, rows=ROWS, cols=COLS, apart=APART):
    layers = weights[0].shape[0]
    groups = layers * rows * cols
    full, own = [], []
    for w in weights:
        lines = w.shape[1] // (2 * Y * Z * rows)
        full.append((layers, Y, Z, 2, rows, lines, w.shape[2]))
        own.append((layers, rows, lines, w.shape[2]))
    halves = (2, *full[0][:3], *full[0][4:]), (*full[2][:3], *full[2][4:])
    a, b = ((s[-2], s[-1] // cols) for s in (full[0], full[2]))
    bf16, dma = jnp.bfloat16, pltpu.SemaphoreType.DMA
    anywhere, vmem = pl.BlockSpec(memory_space=pl.ANY), pl.BlockSpec(memory_space=pltpu.VMEM)
    held = pl.pallas_call(
        functools.partial(kernel, groups, rows, cols, apart),
        out_shape=[pltpu.VMEM(s, bf16) for s in halves] * 2
        + [pltpu.HBM(s, jnp.float32) for s in own] * 2,
        in_specs=[anywhere] * 12,
        out_specs=[vmem] * 4 + [pl.BlockSpec(memory_space=pltpu.HBM)] * 6,
        scratch_shapes=[
            pltpu.VMEM((ACC, 2, Y, Z, *a), bf16),
            pltpu.VMEM((ACC, Y, Z, *b), bf16),
            pltpu.VMEM((Y_SLOTS, 2, Z, *a), bf16),
            pltpu.VMEM((DOWN_SLOTS, *b), bf16),
            pltpu.VMEM((2, *a), bf16),
            pltpu.VMEM((UP_SLOTS, 2, Z - 1, 2, *a), bf16),
            pltpu.VMEM((DOWN_SLOTS, 2, Z - 1, Y, *b), bf16),
            pltpu.VMEM((2, 2, Z - 1, Y, *a), bf16),
            pltpu.VMEM((STAGED, 2, *a), bf16),
            pltpu.VMEM((STAGED, *b), bf16),
            *[pltpu.VMEM((STAGED, *s), jnp.float32) for _ in range(2) for s in ((2, *a), b)],
            dma((4, 3)),
            dma((4, 3)),
            dma((SLOTS, 3)),
            dma((2, 3)),
            dma((SLOTS, 3)),
            dma((2, 3, 2, Z - 1)),
            dma((SLOTS, 3, 2, Z - 1)),
            dma((2, 3, 2, Z - 1)),
            dma((SLOTS, 3, 2, Z - 1)),
            dma((2, Z + 2)),
            dma((SLOTS, Z + 2)),
            dma((2, 4)),
            dma((SLOTS, 4)),
            dma((STAGED, 9)),
            dma((STAGED, 6)),
        ],
        compiler_params=pltpu.CompilerParams(collective_id=0, has_side_effects=True, vmem_limit_bytes=VMEM_BYTES),
        name="sum_step_spread",
    )(
        *[in_hbm(t.reshape(s)) for t, s in zip(terms, full, strict=True)],
        *[in_hbm(w.reshape(s)) for w, s in zip(weights, full, strict=True)],
        *[in_hbm(x.reshape(s)) for x, s in zip(m, own, strict=True)],
        *[in_hbm(x.reshape(s)) for x, s in zip(v, own, strict=True)],
    )
    out = pl.pallas_call(
        put,
        out_shape=[jax.ShapeDtypeStruct(s, bf16) for s in full] + [jax.ShapeDtypeStruct(s, jnp.float32) for s in own] * 2,
        in_specs=[vmem] * 4 + [anywhere] * 6,
        out_specs=[anywhere] * 9,
        scratch_shapes=[*[pltpu.VMEM(s, jnp.float32) for s in own] * 2, dma((12 + 6 * layers,))],
        compiler_params=pltpu.CompilerParams(vmem_limit_bytes=PUT_BYTES),
        name="put",
    )(*held[:4], *[in_hbm(x) for x in held[4:]])
    return (
        *[o.reshape(w.shape) for o, w in zip(out[:3], weights, strict=True)],
        *[o.reshape(x.shape) for o, x in zip(out[3:6], m, strict=True)],
        *[o.reshape(x.shape) for o, x in zip(out[6:], v, strict=True)],
    )


def solution(mesh):
    def step(*arrays):
        terms, weights, m, v = (arrays[i : i + 3] for i in (0, 3, 6, 9))
        return update([t[0] for t in terms], weights, m, v)

    all_of, cut = P(None, None, None), P(None, "dp", None)
    return jax.shard_map(
        step,
        mesh=mesh,
        in_specs=(P(("rep", "dp"), None, None, None),) * 3 + (all_of,) * 3 + (cut,) * 6,
        out_specs=(P("rep", None, None),) * 3 + (P("rep", "dp", None),) * 6,
        check_vma=False,
    )
```

time: 760 us -> 336 us (0.44)
  waiting for transfers between devices: 707 us -> 0 us
  Pallas kernels: 0 us -> 335 us
  local copies, waits for them, and re-layouts: 26 us -> 0 us
  between operations: 14.2 us -> 0.65 us
  other arithmetic: 12.3 us -> 0 us
    reduce_scatter x3 -> x0, waiting for transfers between devices: 404 us -> none  [step(): lax.psum_scatter(t[0], 'dp', scatter_dimension=1, tiled=True)]
    pallas_call x0 -> x2, Pallas kernels: none -> 335 us  [the longest x1 317 us: update(): pl.pallas_call(functools.partial(kernel, groups, rows, cols, apart), out_...]
    all_gather x3 -> x0, waiting for transfers between devices: 301 us -> none  [step(): whole = [lax.all_gather(one[0], 'dp', axis=1, tiled=True) for one in new]]
    unnamed x19 -> x0, local copies, waits for them, and re-layouts: 26 us -> none
    convert_element_type x3 -> x0, other arithmetic: 12.3 us -> none  [adamw(): return ((w - 0.02 * step).astype(jnp.bfloat16), m, v)]
  transfers between devices with their start and end apart: 6 -> 0, of which waited for: 6 -> 0; matrix products, arithmetic and copies ran while one was open for 2% -> 0% of each run, Pallas kernels for 0% -> 0%
where the time goes in v2:
time: 336 us
  Pallas kernels  335 us (100%)
    pallas_call x1, Pallas kernels, update(): pl.pallas_call(functools.partial(kernel, groups, rows, cols, apart), out_...  317 us
    pallas_call x1, Pallas kernels, update(): pl.pallas_call(put, out_shape=[jax.ShapeDtypeStruct(s, bf16) for s in ful...  18 us

profile of v2, /device:TPU:0, one launch (start us, length us, event | category | flops | bytes accessed | tf_op | source)
XLA Modules:
  0.0 335.9 jit_solution(12138241218078722010)
XLA Ops:
  0.6 317.3 %sum_step_spread.1 = (bf16[2,2,2,4,8,8,3072]{6,5,4,3,2,1,0:T(8,128)(2,1)S(1)}, bf16[2,2,4,8,24,1024]{5,4,3,2,1,0:T(8,128)(2,1)S(1)}, bf16[2,2,2,4,8,8,3072]{6,5,...) custom-call(bf16[2,2,4,2,8,8,3072]{6,5,4,3,2,1,0:T(8,128)(2,1)} %bit, ...), custom_call_target="tpu_custom_call" | custom-call | tf_op jit(solution)/shard_map/sum_step_spread/pallas_call | solution.py:429
  317.9 18.0 %put.1 = (bf16[2,2,4,2,8,8,3072]{6,5,4,3,2,1,0:T(8,128)(2,1)}, bf16[2,2,4,2,8,8,3072]{6,5,4,3,2,1,0:T(8,128)(2,1)}, bf16[2,2,4,2,8,24,1024]{6,5,4,3,2,1,0:T(8,12...) custom-call(bf16[2,2,2,4,8,8,3072]{6,5,4,3,2,1,0:T(8,128)(2,1)S(1)} , ...), custom_call_target="tpu_custom_call" | custom-call | tf_op jit(solution)/shard_map/put/pallas_call | solution.py:471

commit v3 on v2

--- a/solution.py
+++ b/solution.py
@@ -10,15 +10,13 @@
 MESH = pl.DeviceIdType.MESH
 Y, Z = 2, 4
 ROWS, COLS = 8, 2
-ACC = 6
 SLOTS = 10
 Y_SLOTS, UP_SLOTS, DOWN_SLOTS = 9, 5, 7
 STAGED = 4
 STAGES = 10
 PAIR, DOWN, GATE, UP = range(4)
 APART = (0, 10, 16, 22)
-VMEM_BYTES = 13 * 2**20
-PUT_BYTES = 13 * 2**20
+VMEM_BYTES = 8 * 2**20
 ORDER = (
     (0, 1), (1, 1), (1, 2), (0, 8), (1, 3), (1, 4), (0, 7), (0, 10), (0, 9), (1, 9), (1, 8), (0, 4), (1, 7), (1, 10), (1, 5), (0, 6), (0, 3), (1, 6), (0, 5), (0, 2),
 )
@@ -27,10 +25,10 @@
 def kernel(groups, rows, cols, apart, *refs):
     terms, weights, moments_m, moments_v = (refs[i : i + 3] for i in (0, 3, 6, 9))
     mine_a, mine_b, theirs_a, theirs_b = refs[12:16]
-    new_m, new_v = refs[16:19], refs[19:22]
-    acc_a, acc_b, y_a, y_b, y_c, z_a, z_b, z_c, w_a, w_b, m_a, m_b, v_a, v_b = refs[22:36]
-    load_sem, pair_send, pair_recv, y_send, y_recv, z_send, z_recv, spread_send, spread_recv = refs[36:45]
-    back_send, back_recv, out_send, out_recv, state_sem, keep_sem = refs[45:51]
+    m_a, m_b, v_a, v_b = refs[16:20]
+    y_a, y_b, y_c, z_a, z_b, z_c, w_a, w_b = refs[20:28]
+    load_sem, pair_send, pair_recv, y_send, y_recv, z_send, z_recv, spread_send, spread_recv = refs[28:37]
+    back_send, back_recv, out_send, out_recv, state_sem, free_sem = refs[37:43]
 
     rep, me = lax.axis_index("rep"), lax.axis_index("dp")
     c = lax.rem(me, 2)
@@ -71,25 +69,27 @@
         return (layer, i, t, h, slice(None), width) if weight == 2 else (weight, layer, i, t, h, slice(None), width)
 
     def acc_at(g, kind, *at):
-        slot = lax.rem(g, ACC)
-        return acc_b.at[slot, *at] if kind == DOWN else acc_a.at[slot, which(kind), *at]
+        return new_at(g, kind, *at, theirs=True)
 
     def summed(g, weight, i, t):
-        slot, here = lax.rem(g, ACC), new_index(g, weight, i, t)
+        here = new_index(g, weight, i, t)
+        return f32(theirs_b[here]) + f32(mine_b[here]) if weight == 2 else f32(theirs_a[here]) + f32(mine_a[here])
+
+    def keep(g, weight, i, t, total):
         if weight == 2:
-            return f32(acc_b[slot, i, t]) + f32(mine_b[here])
-        return f32(acc_a[slot, weight, i, t]) + f32(mine_a[here])
-
-    def keep(g, weight, i, t, total):
-        slot = lax.rem(g, ACC)
-        if weight == 2:
-            acc_b[slot, i, t] = total.astype(jnp.bfloat16)
+            theirs_b[new_index(g, weight, i, t)] = total.astype(jnp.bfloat16)
         else:
-            acc_a[slot, weight, i, t] = total.astype(jnp.bfloat16)
+            theirs_a[new_index(g, weight, i, t)] = total.astype(jnp.bfloat16)
+
+    def tell_partner(kind):
+        pl.semaphore_signal(free_sem.at[kind % 2 + kind // 3], inc=1, device_id=(rep, partner), device_id_type=MESH)
+
+    def hear_partner(kind):
+        pl.semaphore_wait(free_sem.at[kind % 2 + kind // 3], 1)
 
     def own_load(g, k):
         layer, h, width = part(g, terms[k])
-        dst = acc_b.at[lax.rem(g, ACC)] if k == 2 else acc_a.at[lax.rem(g, ACC), k]
+        dst = theirs_b.at[layer, :, :, h, :, width] if k == 2 else theirs_a.at[k, layer, :, :, h, :, width]
         return pltpu.make_async_copy(terms[k].at[layer, :, :, c, h, :, width], dst, load_sem.at[lax.rem(g, 4), k])
 
     def pair_copy(g, k):
@@ -108,7 +108,7 @@
         if z_first(kind):
             src, dst = acc_at(g, kind, 1 - y, z), (y_b if kind == DOWN else y_c).at[slot_of(g, kind)]
         else:
-            src, dst = acc_at(g, kind, 1 - y), y_a.at[lax.rem(g, Y_SLOTS), which(kind)]
+            src, dst = acc_at(g, kind, 1 - y, slice(None)), y_a.at[lax.rem(g, Y_SLOTS), which(kind)]
         i = kind % 2 + kind // 3
         return send_to(across, src, dst, y_send.at[lax.rem(g, 2), i], y_recv.at[slot, i])
 
@@ -144,7 +144,9 @@
 
     def staged(g, k):
         slot = lax.rem(g, STAGED)
-        return (w_b.at[slot], m_b.at[slot], v_b.at[slot]) if k == 2 else (w_a.at[slot, k], m_a.at[slot, k], v_a.at[slot, k])
+        layer, h, width = part(g, moments_m[k])
+        at = (layer, h, slice(None), width) if k == 2 else (k, layer, h, slice(None), width)
+        return (w_b.at[slot], m_b.at[at], v_b.at[at]) if k == 2 else (w_a.at[slot, k], m_a.at[at], v_a.at[at])
 
     def state_loads(g, some):
         slot, copies = lax.rem(g, STAGED), []
@@ -155,15 +157,6 @@
             copies.append(pltpu.make_async_copy(moments_m[k].at[layer, h, :, width], m_ref, state_sem.at[slot, 3 * k + 1]))
             copies.append(pltpu.make_async_copy(moments_v[k].at[layer, h, :, width], v_ref, state_sem.at[slot, 3 * k + 2]))
         return copies
-
-    def state_stores(g, k):
-        layer, h, width = part(g, moments_m[k])
-        _, m_ref, v_ref = staged(g, k)
-        sems = keep_sem.at[lax.rem(g, STAGED), 2 * k], keep_sem.at[lax.rem(g, STAGED), 2 * k + 1]
-        return (
-            pltpu.make_async_copy(m_ref, new_m[k].at[layer, h, :, width], sems[0]),
-            pltpu.make_async_copy(v_ref, new_v[k].at[layer, h, :, width], sems[1]),
-        )
 
     def z_step(g, kind, s):
         slot = slot_of(g, kind)
@@ -268,18 +261,13 @@
                 adamw(g, i, summed(g, i, y, z) + f32(y_a[lax.rem(g, Y_SLOTS), i, z]) + along_z(z_a, g, kind, i))
             spread_step(g, kind, 0)
             back_copy(g, kind, y, z).start()
-            for i in some:
-                for copy in state_stores(g, i):
-                    copy.start()
+            tell_partner(kind)
         if k in (6, 7):
             spread_wait(g, kind, k - 6)
             spread_step(g, kind, k - 5)
-        if k == 6:
-            for i in some:
-                for copy in state_stores(g, i):
-                    copy.wait()
         if k == 8:
             spread_wait(g, kind, 2)
+            hear_partner(kind)
             out_copy(g, kind, 0).start()
         if k == 9:
             for t in range(Z):
@@ -311,19 +299,17 @@
             arrived = f32((y_b if kind == DOWN else y_c)[slot_of(g, kind)])
             adamw(g, weight, summed(g, weight, y, z) + arrived + along_z(came, g, kind, y))
             back_copy(g, kind, y, z).start()
-            for copy in state_stores(g, weight):
-                copy.start()
+            tell_partner(kind)
         if k == 6:
             back_copy(g, kind, 1 - y, z).wait_recv()
             back_copy(g, kind, y, z).wait_send()
             spread_step(g, kind, 0)
-            for copy in state_stores(g, weight):
-                copy.wait()
         if k in (7, 8):
             spread_wait(g, kind, k - 7)
             spread_step(g, kind, k - 6)
         if k == 9:
             spread_wait(g, kind, 2)
+            hear_partner(kind)
             out_copy(g, kind, 0).start()
         if k == 10:
             out_copy(g, kind, 0).wait()
@@ -390,23 +376,20 @@
 
 
 def put(*refs):
-    halves, moments = (refs[0:2], refs[2:4]), refs[4:10]
-    outs, rooms, sem = refs[10:19], refs[19:25], refs[25]
+    halves, moments = (refs[0:2], refs[2:4]), (refs[4:6], refs[6:8])
+    outs, sem = refs[8:17], refs[17]
     c = lax.rem(lax.axis_index("dp"), 2)
     pairs = []
     for core, (a, b) in zip((c, 1 - c), halves, strict=True):
         for layer in range(b.shape[0]):
             sources = a.at[0, layer], a.at[1, layer], b.at[layer]
             pairs += [(src, out.at[layer, :, :, core]) for src, out in zip(sources, outs[:3], strict=True)]
-    came = [pltpu.make_async_copy(src, room, sem.at[n]) for n, (src, room) in enumerate(zip(moments, rooms, strict=True))]
-    gone = [pltpu.make_async_copy(room, out, sem.at[6 + n]) for n, (room, out) in enumerate(zip(rooms, outs[3:], strict=True))]
-    copies = [pltpu.make_async_copy(src, dst, sem.at[12 + n]) for n, (src, dst) in enumerate(pairs)]
-    for copy in came + copies:
+    for i, (a, b) in enumerate(moments):
+        pairs += zip((a.at[0], a.at[1], b), outs[3 + 3 * i : 6 + 3 * i], strict=True)
+    copies = [pltpu.make_async_copy(src, dst, sem.at[n]) for n, (src, dst) in enumerate(pairs)]
+    for copy in copies:
         copy.start()
-    for first, then in zip(came, gone, strict=True):
-        first.wait()
-        then.start()
-    for copy in copies + gone:
+    for copy in copies:
         copy.wait()
 
 
@@ -429,12 +412,10 @@
     held = pl.pallas_call(
         functools.partial(kernel, groups, rows, cols, apart),
         out_shape=[pltpu.VMEM(s, bf16) for s in halves] * 2
-        + [pltpu.HBM(s, jnp.float32) for s in own] * 2,
+        + [pltpu.VMEM(s, jnp.float32) for s in ((2, *own[0]), own[2])] * 2,
         in_specs=[anywhere] * 12,
-        out_specs=[vmem] * 4 + [pl.BlockSpec(memory_space=pltpu.HBM)] * 6,
+        out_specs=[vmem] * 8,
         scratch_shapes=[
-            pltpu.VMEM((ACC, 2, Y, Z, *a), bf16),
-            pltpu.VMEM((ACC, Y, Z, *b), bf16),
             pltpu.VMEM((Y_SLOTS, 2, Z, *a), bf16),
             pltpu.VMEM((DOWN_SLOTS, *b), bf16),
             pltpu.VMEM((2, *a), bf16),
@@ -443,7 +424,6 @@
             pltpu.VMEM((2, 2, Z - 1, Y, *a), bf16),
             pltpu.VMEM((STAGED, 2, *a), bf16),
             pltpu.VMEM((STAGED, *b), bf16),
-            *[pltpu.VMEM((STAGED, *s), jnp.float32) for _ in range(2) for s in ((2, *a), b)],
             dma((4, 3)),
             dma((4, 3)),
             dma((SLOTS, 3)),
@@ -458,7 +438,7 @@
             dma((2, 4)),
             dma((SLOTS, 4)),
             dma((STAGED, 9)),
-            dma((STAGED, 6)),
+            pltpu.SemaphoreType.REGULAR((3,)),
         ],
         compiler_params=pltpu.CompilerParams(collective_id=0, has_side_effects=True, vmem_limit_bytes=VMEM_BYTES),
         name="sum_step_spread",
@@ -471,12 +451,12 @@
     out = pl.pallas_call(
         put,
         out_shape=[jax.ShapeDtypeStruct(s, bf16) for s in full] + [jax.ShapeDtypeStruct(s, jnp.float32) for s in own] * 2,
-        in_specs=[vmem] * 4 + [anywhere] * 6,
+        in_specs=[vmem] * 8,
         out_specs=[anywhere] * 9,
-        scratch_shapes=[*[pltpu.VMEM(s, jnp.float32) for s in own] * 2, dma((12 + 6 * layers,))],
-        compiler_params=pltpu.CompilerParams(vmem_limit_bytes=PUT_BYTES),
+        scratch_shapes=[dma((6 + 6 * layers,))],
+        compiler_params=pltpu.CompilerParams(vmem_limit_bytes=VMEM_BYTES),
         name="put",
-    )(*held[:4], *[in_hbm(x) for x in held[4:]])
+    )(*held)
     return (
         *[o.reshape(w.shape) for o, w in zip(out[:3], weights, strict=True)],
         *[o.reshape(x.shape) for o, x in zip(out[3:6], m, strict=True)],

time: 336 us -> 333 us (level)
  no operation moved by 1% of the time
where the time goes in v3:
time: 333 us
  Pallas kernels  332 us (100%)
    pallas_call x1, Pallas kernels, update(): pl.pallas_call(functools.partial(kernel, groups, rows, cols, apart), out_...  317 us
    pallas_call x1, Pallas kernels, update(): pl.pallas_call(put, out_shape=[jax.ShapeDtypeStruct(s, bf16) for s in ful...  15.2 us

profile of v3, /device:TPU:0, one launch (start us, length us, event | category | flops | bytes accessed | tf_op | source)
XLA Modules:
  0.0 333.0 jit_solution(3026947225329131182)
XLA Ops:
  0.6 317.1 %sum_step_spread.1 = (bf16[2,2,2,4,8,8,3072]{6,5,4,3,2,1,0:T(8,128)(2,1)S(1)}, bf16[2,2,4,8,24,1024]{5,4,3,2,1,0:T(8,128)(2,1)S(1)}, bf16[2,2,2,4,8,8,3072]{6,5,...) custom-call(bf16[2,2,4,2,8,8,3072]{6,5,4,3,2,1,0:T(8,128)(2,1)} %bit, ...), custom_call_target="tpu_custom_call" | custom-call | tf_op jit(solution)/shard_map/sum_step_spread/pallas_call | solution.py:412
  317.7 15.2 %put.1 = (bf16[2,2,4,2,8,8,3072]{6,5,4,3,2,1,0:T(8,128)(2,1)}, bf16[2,2,4,2,8,8,3072]{6,5,4,3,2,1,0:T(8,128)(2,1)}, bf16[2,2,4,2,8,24,1024]{6,5,4,3,2,1,0:T(8,12...) custom-call(bf16[2,2,2,4,8,8,3072]{6,5,4,3,2,1,0:T(8,128)(2,1)S(1)} , ...), custom_call_target="tpu_custom_call" | custom-call | tf_op jit(solution)/shard_map/put/pallas_call | solution.py:451

commit v4 on v3

--- a/solution.py
+++ b/solution.py
@@ -14,11 +14,12 @@
 Y_SLOTS, UP_SLOTS, DOWN_SLOTS = 9, 5, 7
 STAGED = 4
 STAGES = 10
+BY_BLOCK = 3
 PAIR, DOWN, GATE, UP = range(4)
-APART = (0, 10, 16, 22)
+APART = (0, 7, 11, 17, 21)
 VMEM_BYTES = 8 * 2**20
 ORDER = (
-    (0, 1), (1, 1), (1, 2), (0, 8), (1, 3), (1, 4), (0, 7), (0, 10), (0, 9), (1, 9), (1, 8), (0, 4), (1, 7), (1, 10), (1, 5), (0, 6), (0, 3), (1, 6), (0, 5), (0, 2),
+    (1, 7), (1, 5), (1, 6), (1, 4), (0, 8), (0, 7), (1, 3), (1, 9), (1, 8), (0, 1), (0, 9), (0, 6), (1, 2), (1, 10), (0, 10), (0, 5), (1, 1), (0, 4), (0, 3), (0, 2),
 )
 
 
@@ -131,9 +132,9 @@
         sems = spread_send.at[lax.rem(g, 2), i, way, s], spread_recv.at[lax.rem(g, SLOTS), i, way, s]
         return send_to(beside[way], ref, ref, *sems)
 
-    def back_copy(g, kind, i, t):
-        ref = new_at(g, kind, i, t)
-        at = Z + kind // 3 if z_first(kind) else t
+    def back_copy(g, kind, i, t=None):
+        ref = new_at(g, kind, i, slice(None) if t is None else t)
+        at = Z + kind // 3 if z_first(kind) else Z + 2 if t is None else t
         return send_to(across, ref, ref, back_send.at[lax.rem(g, 2), at], back_recv.at[lax.rem(g, SLOTS), at])
 
     def out_copy(g, kind, half):
@@ -212,7 +213,11 @@
                 t = z - 1 - s if way == 0 else z + 1 + s
                 spread_copy(g, kind, way, s, t).wait_recv()
                 if not z_first(kind):
-                    back_copy(g, kind, y, t).start()
+
+                    @pl.when(g >= groups - BY_BLOCK)
+                    def _():
+                        back_copy(g, kind, y, t).start()
+
 
             @pl.when((place[way] >= s) & (place[way] < Z - 1))
             def _(way=way):
@@ -260,19 +265,37 @@
             for i in some:
                 adamw(g, i, summed(g, i, y, z) + f32(y_a[lax.rem(g, Y_SLOTS), i, z]) + along_z(z_a, g, kind, i))
             spread_step(g, kind, 0)
-            back_copy(g, kind, y, z).start()
+
+            @pl.when(g >= groups - BY_BLOCK)
+            def _():
+                back_copy(g, kind, y, z).start()
+
             tell_partner(kind)
         if k in (6, 7):
             spread_wait(g, kind, k - 6)
             spread_step(g, kind, k - 5)
         if k == 8:
             spread_wait(g, kind, 2)
+
+            @pl.when(g < groups - BY_BLOCK)
+            def _():
+                back_copy(g, kind, y).start()
+
             hear_partner(kind)
             out_copy(g, kind, 0).start()
         if k == 9:
-            for t in range(Z):
-                back_copy(g, kind, 1 - y, t).wait_recv()
-                back_copy(g, kind, y, t).wait_send()
+
+            @pl.when(g < groups - BY_BLOCK)
+            def _():
+                back_copy(g, kind, 1 - y).wait_recv()
+                back_copy(g, kind, y).wait_send()
+
+            @pl.when(g >= groups - BY_BLOCK)
+            def _():
+                for t in range(Z):
+                    back_copy(g, kind, 1 - y, t).wait_recv()
+                    back_copy(g, kind, y, t).wait_send()
+
             out_copy(g, kind, 1).start()
         if k == 10:
             for half in (0, 1):
@@ -433,8 +456,8 @@
             dma((SLOTS, 3, 2, Z - 1)),
             dma((2, 3, 2, Z - 1)),
             dma((SLOTS, 3, 2, Z - 1)),
-            dma((2, Z + 2)),
-            dma((SLOTS, Z + 2)),
+            dma((2, Z + 3)),
+            dma((SLOTS, Z + 3)),
             dma((2, 4)),
             dma((SLOTS, 4)),
             dma((STAGED, 9)),

time: 333 us -> 330 us (level)
  no operation moved by 1% of the time
where the time goes in v4:
time: 330 us
  Pallas kernels  329 us (100%)
    pallas_call x1, Pallas kernels, update(): pl.pallas_call(functools.partial(kernel, groups, rows, cols, apart), out_...  314 us
    pallas_call x1, Pallas kernels, update(): pl.pallas_call(put, out_shape=[jax.ShapeDtypeStruct(s, bf16) for s in ful...  15.2 us

profile of v4, /device:TPU:0, one launch (start us, length us, event | category | flops | bytes accessed | tf_op | source)
XLA Modules:
  0.0 330.1 jit_solution(6809479434056487945)
XLA Ops:
  0.6 314.2 %sum_step_spread.1 = (bf16[2,2,2,4,8,8,3072]{6,5,4,3,2,1,0:T(8,128)(2,1)S(1)}, bf16[2,2,4,8,24,1024]{5,4,3,2,1,0:T(8,128)(2,1)S(1)}, bf16[2,2,2,4,8,8,3072]{6,5,...) custom-call(bf16[2,2,4,2,8,8,3072]{6,5,4,3,2,1,0:T(8,128)(2,1)} %bit, ...), custom_call_target="tpu_custom_call" | custom-call | tf_op jit(solution)/shard_map/sum_step_spread/pallas_call | solution.py:435
  314.9 15.2 %put.1 = (bf16[2,2,4,2,8,8,3072]{6,5,4,3,2,1,0:T(8,128)(2,1)}, bf16[2,2,4,2,8,8,3072]{6,5,4,3,2,1,0:T(8,128)(2,1)}, bf16[2,2,4,2,8,24,1024]{6,5,4,3,2,1,0:T(8,12...) custom-call(bf16[2,2,2,4,8,8,3072]{6,5,4,3,2,1,0:T(8,128)(2,1)S(1)} , ...), custom_call_target="tpu_custom_call" | custom-call | tf_op jit(solution)/shard_map/put/pallas_call | solution.py:474

commit v5 on v4

--- a/solution.py
+++ b/solution.py
@@ -14,9 +14,9 @@
 Y_SLOTS, UP_SLOTS, DOWN_SLOTS = 9, 5, 7
 STAGED = 4
 STAGES = 10
-BY_BLOCK = 3
+BY_BLOCK = 2
 PAIR, DOWN, GATE, UP = range(4)
-APART = (0, 7, 11, 17, 21)
+APART = (0, 6, 10, 15, 20)
 VMEM_BYTES = 8 * 2**20
 ORDER = (
     (1, 7), (1, 5), (1, 6), (1, 4), (0, 8), (0, 7), (1, 3), (1, 9), (1, 8), (0, 1), (0, 9), (0, 6), (1, 2), (1, 10), (0, 10), (0, 5), (1, 1), (0, 4), (0, 3), (0, 2),
@@ -349,6 +349,10 @@
         for k in range(3):
             own_load(g, k).start()
 
+    for g in (0, 1):
+        for k in range(3):
+            own_load(g, k).start()
+
     barrier = pltpu.get_barrier_semaphore()
     for device in (partner, across):
         pl.semaphore_signal(barrier, inc=1, device_id=(rep, device), device_id_type=MESH)
@@ -360,8 +364,9 @@
 
     pl.semaphore_wait(barrier, 4 - jnp.where(z == 0, 1, 0) - jnp.where(far == 0, 1, 0))
 
-    enter(0)
-    enter(1)
+    for g in (0, 1):
+        for k in range(3):
+            pair_copy(g, k).start()
 
     @pl.loop(0, groups + STAGES - 1)
     def _(tick):

time: 330 us -> 330 us (level)
  no operation moved by 1% of the time
where the time goes in v5:
time: 330 us
  Pallas kernels  329 us (100%)
    pallas_call x1, Pallas kernels, update(): pl.pallas_call(functools.partial(kernel, groups, rows, cols, apart), out_...  314 us
    pallas_call x1, Pallas kernels, update(): pl.pallas_call(put, out_shape=[jax.ShapeDtypeStruct(s, bf16) for s in ful...  15.2 us

profile of v5, /device:TPU:0, one launch (start us, length us, event | category | flops | bytes accessed | tf_op | source)
XLA Modules:
  0.0 329.9 jit_solution(13132325302136982979)
XLA Ops:
  0.6 314.1 %sum_step_spread.1 = (bf16[2,2,2,4,8,8,3072]{6,5,4,3,2,1,0:T(8,128)(2,1)S(1)}, bf16[2,2,4,8,24,1024]{5,4,3,2,1,0:T(8,128)(2,1)S(1)}, bf16[2,2,2,4,8,8,3072]{6,5,...) custom-call(bf16[2,2,4,2,8,8,3072]{6,5,4,3,2,1,0:T(8,128)(2,1)} %bit, ...), custom_call_target="tpu_custom_call" | custom-call | tf_op jit(solution)/shard_map/sum_step_spread/pallas_call | solution.py:440
  314.7 15.2 %put.1 = (bf16[2,2,4,2,8,8,3072]{6,5,4,3,2,1,0:T(8,128)(2,1)}, bf16[2,2,4,2,8,8,3072]{6,5,4,3,2,1,0:T(8,128)(2,1)}, bf16[2,2,4,2,8,24,1024]{6,5,4,3,2,1,0:T(8,12...) custom-call(bf16[2,2,2,4,8,8,3072]{6,5,4,3,2,1,0:T(8,128)(2,1)S(1)} , ...), custom_call_target="tpu_custom_call" | custom-call | tf_op jit(solution)/shard_map/put/pallas_call | solution.py:479
